TPU v7x, 32 devices: a whole 2x2x4 slice. The times are simulated.
32 devices in a mesh: row: 4 (over x, core), col: 4 (over z), inner: 2 (over y).
Axes of the slice: x: 2, y: 2, z: 4, core: 2. Of those that a mesh axis runs over, the one named last changes fastest.
Arguments:
- near_flags: int32 [4, 6], P('row', 'inner'), may hold values 0 or 1
- row_factor: bfloat16 [4, 6, 64, 2048], P('row', 'inner', None, 'col'), may hold values from -6 to 6
- col_factor: bfloat16 [4, 6, 64, 2048], P('row', 'inner', None, 'col'), may hold values from -0.0068359375 to 0.0068359375
- near_block: bfloat16 [4, 6, 2048, 2048], P('row', 'inner', None, 'col'), may hold values from -0.0546875 to 0.0546875
- inner_left: bfloat16 [6, 16, 64, 2048], P('inner', 'col', None, 'row'), may hold values from -6 to 6
- inner_right: bfloat16 [6, 16, 64, 2048], P('inner', 'col', None, 'row'), may hold values from -0.75 to 0.75
- sketch_matrix: bfloat16 [16, 64, 2048], P('col'), may hold values from -0.125 to 0.125
Outputs:
- basis: float32 [4, 16, 64, 2048], P('row', 'col', None, 'inner')
- coupling: float32 [4, 16, 64, 2048], P('row', 'col', None, 'inner')
Inputs may be any that keep to these rules, and one draw needn't show every extreme that they name: `near_flags`: 1 marks a near-field block.
All inputs are finite; a program needn't handle non-finite values.
Results may differ from a plain program's by a relative error of at most 0.0055.
Values may be sent and summed in bfloat16 or wider, within the bound.
A program may use at most 128 MiB of HBM per device.

v0:
```python
import math

import jax
import jax.numpy as jnp
from jax import lax
from jax.sharding import PartitionSpec as P

L = 2048
R = 64


def solve_lower(lower, sampled):
    return jax.scipy.linalg.solve_triangular(lower, sampled, lower=True)


def cholesky_basis(gram_matrix, sampled):
    lower = jnp.linalg.cholesky(gram_matrix)
    return jax.vmap(solve_lower)(lower, sampled)


def gram_of(sampled):
    return jnp.einsum("jsl,jtl->jst", sampled, sampled, precision=lax.Precision.HIGHEST) / L


def local(near_flags, row_factor, col_factor, near_block, inner_left, inner_right, sketch_matrix):
    wide = jnp.float32
    narrow = jnp.bfloat16
    highest = lax.Precision.HIGHEST
    left_full, right_full = (
        lax.all_gather(inner_left, "row", axis=3, tiled=True),
        lax.all_gather(inner_right, "row", axis=3, tiled=True),
    )
    nearness = near_flags[0]
    slots = left_full.shape[0]
    pieces = []
    cols_full = lax.all_gather(col_factor[0], "col", axis=2, tiled=True)
    left_all = lax.all_gather(left_full, "col", axis=1, tiled=True)
    rows_local = row_factor[0]
    blocks_local = near_block[0]
    every_column = left_all.shape[1]
    local_rows = rows_local.shape[-1]
    for slot in range(slots):

        def lowrank():
            coupled = jnp.einsum(
                "rl,jsl->jrs", cols_full[slot], left_all[slot], preferred_element_type=wide
            ).astype(narrow)
            return jnp.einsum("jrs,rl->jsl", coupled, rows_local[slot], preferred_element_type=wide)

        def neardense():
            flat = left_all[slot].reshape(every_column * R, L)
            return jnp.dot(flat, blocks_local[slot], preferred_element_type=wide).reshape(
                every_column, R, local_rows
            )

        pieces.append(lax.cond(nearness[slot] > 0, neardense, lowrank).astype(narrow))
    pieces = lax.all_to_all(jnp.stack(pieces), "col", split_axis=1, concat_axis=3, tiled=True)
    reduced = jnp.einsum(
        "kjrl,jsl->kjrs", right_full, sketch_matrix, preferred_element_type=wide
    ).astype(narrow)
    sampled_part = jnp.einsum("kjrs,kjrl->jsl", reduced, pieces, preferred_element_type=wide)
    share = L // lax.axis_size("inner")
    sampled = lax.psum(sampled_part, "inner")
    basis = cholesky_basis(gram_of(sampled), sampled)
    basis_own = lax.dynamic_slice_in_dim(basis, lax.axis_index("inner") * share, share, 2)
    projected = jnp.einsum(
        "kjrl,jsl->kjrs", pieces.astype(wide), basis, precision=highest
    ) / math.sqrt(L)
    coupling_part = jnp.einsum(
        "kjrs,kjrl->jsl", projected, right_full.astype(wide), precision=highest
    )
    coupling = lax.psum_scatter(coupling_part, "inner", scatter_dimension=2, tiled=True)
    return (basis_own[None], coupling[None])


def solution(mesh):
    in_specs = (
        P("row", "inner"),
        P("row", "inner", None, "col"),
        P("row", "inner", None, "col"),
        P("row", "inner", None, "col"),
        P("inner", "col", None, "row"),
        P("inner", "col", None, "row"),
        P("col", None, None),
    )
    out_specs = (P("row", "col", None, "inner"), P("row", "col", None, "inner"))
    return jax.shard_map(local, mesh=mesh, in_specs=in_specs, out_specs=out_specs, check_vma=False)
```

profile of v0, /device:TPU:24, one launch (start us, length us, event | category | flops | bytes accessed | tf_op | source)
XLA Modules:
  0.0 533.5 jit_solution(14639697719327880574)
XLA Ops:
  8.0 31.1 %all-gather.7.cloned.1.call-done = bf16[3,4,64,2048]{3,2,1,0:T(8,128)(2,1)} async-done(((bf16[3,4,64,512]{3,2,1,0:T(8,128)(2,1)}), bf16[3,4,64,2048]{3,2,1,0:T(8,128)(2,1)}) %all-gather.7.cloned.1.call-update) | async-done | bytes 3145744 | tf_op jit(solution)/shard_map/all_gather | solution.py:30
  41.7 25.4 %all-gather = bf16[1,3,64,2048]{3,2,1,0:T(8,128)(2,1)S(1)} all-gather(bf16[1,3,64,512]{3,2,1,0:T(8,128)(2,1)S(1)} %copy-done.8), channel_id=2, replica_groups=mesh['row'=4,'col'=4,'inner'=2] {'col'}, dimensions={3}, use_global_device_ids=true | all-gather | bytes 983040 | tf_op jit(solution)/shard_map/all_gather | solution.py:36
  67.1 194.7 %all-gather.9.cloned.1.call-done = bf16[3,16,64,2048]{3,2,1,0:T(8,128)(2,1)} async-done(((bf16[3,4,64,2048]{3,2,1,0:T(8,128)(2,1)}), bf16[3,16,64,2048]{3,2,1,0:T(8,128)(2,1)}) %all-gather.9.cloned.1.call-update) | async-done | bytes 12582928 | tf_op jit(solution)/shard_map/all_gather | solution.py:37
  261.8 4.1 conditional.4
  261.8 4.1 fusion.33
  265.9 5.0 conditional.3
  266.8 4.1 fusion.10
  270.9 6.2 %conditional.5 = (bf16[16,64,512]{2,1,0:T(8,128)(2,1)}) conditional(s32[]{:T(128)} %bitcast.37, (bf16[3,16,64,2048]{3,2,1,0:T(8,128)(2,1)}, bf16[3,64,2048]{2,1,0:T(8,128)(2,1)}, bf16[3,64,512]{2,1,0:T(8,128)(2,1)S(1)}) %tuple.55, (bf16[3,16,64,2048]{3,2,1,0:T(8,128)(2,1)}, bf16[3,2048,512]{2,1,0:T(8,128)(2,1)}) %tuple.52), branch_computations={%region_4.0_spmd, %region_5.0_spmd} | conditional | flops 2147483648 | bytes 7340040 | solution.py:56
  270.9 6.2 %fusion.64 = bf16[16,64,512]{2,1,0:T(8,128)(2,1)} fusion(bf16[3,16,64,2048]{3,2,1,0:T(8,128)(2,1)} %get-tuple-element.52, bf16[3,2048,512]{2,1,0:T(8,128)(2,1)} %get-tuple-element.53), kind=kOutput, calls=%fused_computation.40 | convolution fusion | flops 2147483648 | bytes 7340032 | tf_op jit(solution)/shard_map/cond/branch_1_fun/dot_general | solution.py:52
  277.1 3.3 pad_maximum_fusion
  280.4 6.4 %all-to-all-start = ((bf16[3,16,64,512]{3,2,0,1:T(8,128)(2,1)}), bf16[3,16,64,512]{3,2,0,1:T(8,128)(2,1)}, u32[]{:S(2)}, u32[]{:S(2)}) async-start(bf16[3,16,64,512]{3,2,0,1:T(8,128)(2,1)} %pad_maximum_fusion), calls=%async_computation | async-start | bytes 6291456 | tf_op jit(solution)/shard_map/all_to_all | solution.py:57
  288.0 67.9 %all-to-all-done = bf16[3,16,64,512]{3,2,0,1:T(8,128)(2,1)} async-done(((bf16[3,16,64,512]{3,2,0,1:T(8,128)(2,1)}), bf16[3,16,64,512]{3,2,0,1:T(8,128)(2,1)}, u32[]{:S(2)}, u32[]{:S(2)}) %all-to-all-start) | async-done | bytes 3145760 | tf_op jit(solution)/shard_map/all_to_all | solution.py:57
  355.8 6.1 %copy.27 = bf16[3,4,4,64,512]{4,1,3,0,2:T(4,128)(2,1)} copy(bf16[3,4,4,64,512]{4,3,0,2,1:T(8,128)(2,1)} %bitcast.39) | data formatting | bytes 6291456 | tf_op jit(solution)/shard_map/all_to_all | solution.py:57
  361.9 6.1 %all_to_all.16 = bf16[3,4,64,2048]{3,2,0,1:T(8,128)(2,1)} reshape(bf16[3,4,64,4,512]{4,3,2,0,1:T(4,128)(2,1)} %bitcast.156) | data formatting | bytes 6291456 | tf_op jit(solution)/shard_map/all_to_all | solution.py:57
  368.0 6.1 %convolution_bitcast_fusion.1 = f32[4,64,2048]{2,1,0:T(8,128)} fusion(bf16[3,4,64,2048]{3,2,0,1:T(8,128)(2,1)} %all_to_all.16, bf16[3,4,64,2048]{3,2,0,1:T(8,128)(2,1)} %all-gather.5.cloned.1.call-done, bf16[4,64,2048]{2,1,0:T(8,128)(2,1)S(1)} %copy-done), kind=kOutput, calls=%fused_computation.48 | convolution fusion | flops 402702336 | bytes 9437184 | tf_op jit(solution)/shard_map/kjrs,kjrl->jsl/dot_general | solution.py:61
  374.2 64.0 %all-reduce.2.cloned.1.call-done = f32[4,64,2048]{2,1,0:T(8,128)} async-done(((f32[4,64,2048]{2,1,0:T(8,128)}), f32[4,64,2048]{2,1,0:T(8,128)}) %all-reduce.2.cloned.1.call-update) | async-done | bytes 2097168 | tf_op jit(solution)/shard_map/psum | solution.py:63
  438.3 4.4 fusion.85
  442.8 23.5 %custom-call.8 = f32[4,64,64]{2,1,0:T(8,128)S(1)} custom-call(f32[4,64,64]{2,1,0:T(8,128)S(1)} %fusion.83), custom_call_target="Cholesky" | custom-call | tf_op jit(solution)/shard_map/jit(cholesky)/cholesky | solution.py:17
  466.5 19.7 %custom-call.9 = f32[4,1,64,64]{2,3,1,0:T(8,128)S(1)} custom-call(f32[4,1,64,64]{3,2,1,0:T(8,128)S(1)} %select_bitcast_fusion), custom_call_target="InvertDiagBlocksLowerTriangular" | custom-call | tf_op jit(solution)/shard_map/vmap(jit(_solve_triangular))/triangular_solve | solution.py:13
  486.2 1.9 fusion.81
  488.2 3.5 fusion.74
  491.6 3.2 convolution_bitcast_fusion
  494.9 2.3 dynamic-slice_bitcast_fusion
  497.2 29.7 %reduce-scatter.2.cloned.1.call-done = f32[4,64,1024]{2,1,0:T(8,128)} async-done(((f32[4,64,2048]{2,1,0:T(8,128)}), f32[4,64,1024]{2,1,0:T(8,128)}) %reduce-scatter.2.cloned.1.call-update) | async-done | bytes 1048592 | tf_op jit(solution)/shard_map/reduce_scatter | solution.py:72
  (42 shorter events, 4.0 us)
Async XLA Ops:
  7.2 360.9 %copy-start = (bf16[4,64,2048]{2,1,0:T(8,128)(2,1)S(1)}, bf16[4,64,2048]{2,1,0:T(8,128)(2,1)}, u32[]{:S(2)}) copy-start(bf16[4,64,2048]{2,1,0:T(8,128)(2,1)} %param.19) | copy-start | bytes 3145732
  7.2 31.9 %copy-start.9 = (s32[1,3]{1,0:T(1,128)S(1)}, s32[1,3]{1,0:T(1,128)}, u32[]{:S(2)}) copy-start(s32[1,3]{1,0:T(1,128)} %param.13) | copy-start | bytes 40
  7.2 34.5 %copy-start.8 = (bf16[1,3,64,512]{3,2,1,0:T(8,128)(2,1)S(1)}, bf16[1,3,64,512]{3,2,1,0:T(8,128)(2,1)}, u32[]{:S(2)}) copy-start(bf16[1,3,64,512]{3,2,1,0:T(8,128)(2,1)} %param.15) | copy-start | bytes 589828
  7.2 254.6 %copy-start.10 = (bf16[1,3,64,512]{3,2,1,0:T(8,128)(2,1)S(1)}, bf16[1,3,64,512]{3,2,1,0:T(8,128)(2,1)}, u32[]{:S(2)}) copy-start(bf16[1,3,64,512]{3,2,1,0:T(8,128)(2,1)} %param.14) | copy-start | bytes 589828
  7.2 31.9 %all-gather.7.cloned.1.call-start = ((), (), s32[]{:S(2)}) async-start(), calls=%async_computation.3 | async-start | bytes 3932160 | tf_op jit(solution)/shard_map/all_gather | solution.py:30
  7.9 253.8 %all-gather.9.cloned.1.call-start = ((), (), s32[]{:S(2)}) async-start(), calls=%async_computation.4 | async-start | bytes 15728640 | tf_op jit(solution)/shard_map/all_gather | solution.py:37
  67.1 198.8 %copy-start.6 = (bf16[1,3,64,2048]{3,2,1,0:T(8,128)(2,1)}, bf16[1,3,64,2048]{3,2,1,0:T(8,128)(2,1)S(1)}, u32[]{:S(2)}) copy-start(bf16[1,3,64,2048]{3,2,1,0:T(8,128)(2,1)S(1)} %all-gather) | copy-start | bytes 2359300
  265.9 0.9 copy-start.7
  280.4 6.4 %copy-start.5 = (bf16[3,4,64,512]{3,2,1,0:T(8,128)(2,1)S(1)}, bf16[3,4,64,512]{3,2,1,0:T(8,128)(2,1)}, u32[]{:S(2)}) copy-start(bf16[3,4,64,512]{3,2,1,0:T(8,128)(2,1)} %param.18) | copy-start | bytes 2359300
  280.4 75.4 %all-to-all-start = ((bf16[3,16,64,512]{3,2,0,1:T(8,128)(2,1)}), bf16[3,16,64,512]{3,2,0,1:T(8,128)(2,1)}, u32[]{:S(2)}, u32[]{:S(2)}) async-start(bf16[3,16,64,512]{3,2,0,1:T(8,128)(2,1)} %pad_maximum_fusion), calls=%async_computation | async-start | bytes 6291456 | tf_op jit(solution)/shard_map/all_to_all | solution.py:57
  286.8 81.3 %all-gather.5.cloned.1.call-start = ((), (), s32[]{:S(2)}) async-start(), calls=%async_computation.2 | async-start | bytes 3932160 | tf_op jit(solution)/shard_map/all_gather | solution.py:31
  287.8 150.5 %all-reduce.2.cloned.1.call-start = ((), (), s32[]{:S(2)}) async-start(), calls=%async_computation.5 | async-start | bytes 4194304 | tf_op jit(solution)/shard_map/psum | solution.py:63
  374.1 152.8 %reduce-scatter.2.cloned.1.call-start = ((), (), s32[]{:S(2)}) async-start(), calls=%async_computation.6 | async-start | bytes 3145728 | tf_op jit(solution)/shard_map/reduce_scatter | solution.py:72
  438.3 47.9 %copy-start.2 = (f32[4,64,2048]{2,1,0:T(8,128)S(1)}, f32[4,64,2048]{2,1,0:T(8,128)}, u32[]{:S(2)}) copy-start(f32[4,64,2048]{2,1,0:T(8,128)} %all-reduce.2.cloned.1.call-done) | copy-start | bytes 6291460
  486.2 1.9 copy-start.1
  488.1 3.5 copy-start.3
  488.1 3.5 copy-start.4
Sparse Core Ops, SparseCore 0:
  9.6 29.4 all-gather.6
  40.7 221.0 all-gather.8
  289.7 29.3 all-gather.4
  374.3 63.9 all-reduce.1
  495.0 31.8 reduce-scatter.1
where the time goes:
time: 535 us; the launch traced here: 533 us
  waiting for transfers between devices  388 us (73%)
  other arithmetic  46.7 us (9%)
  matrix products  33.4 us (6%)
  blocking collectives  25.4 us (5%)
  local copies, waits for them, and re-layouts  17.1 us (3%)
  between operations  15.9 us (3%)
  starting transfers between devices  6.7 us (1%)
    all_gather x1, waiting for transfers between devices, local(): left_all = lax.all_gather(left_full, 'col', axis=1, tiled=True)  195 us
    all_to_all x1, waiting for transfers between devices, local(): lax.all_to_all(jnp.stack(pieces), 'col', split_axis=1, concat_axis=3, til...  67.9 us
    psum x1, waiting for transfers between devices, local(): sampled = lax.psum(sampled_part, 'inner')  64 us
    all_gather x1, waiting for transfers between devices, local(): lax.all_gather(inner_left, 'row', axis=3, tiled=True)  31.1 us
    reduce_scatter x1, waiting for transfers between devices, local(): lax.psum_scatter(coupling_part, 'inner', scatter_dimension=2, tiled=True)  29.7 us
    all_gather x1, blocking collectives, local(): cols_full = lax.all_gather(col_factor[0], 'col', axis=2, tiled=True)  25.4 us
    another operation x4, other arithmetic, cholesky_basis(): lower = jnp.linalg.cholesky(gram_matrix)  23.6 us
    another operation x3, other arithmetic, solve_lower(): return jax.scipy.linalg.solve_triangular(lower, sampled, lower=True)  19.8 us
  transfers between devices with their start and end apart: 6, of which 5 were waited for; matrix products, arithmetic and copies ran while one was open for 2% of the time, Pallas kernels for 0%

commit v1 on v0

v1 whole, which is shorter than its diff:
```python
import functools
import math

import jax
import jax.numpy as jnp
from jax import lax
from jax.experimental import pallas as pl
from jax.experimental.pallas import tpu as pltpu
from jax.sharding import PartitionSpec as P

MESH = pl.DeviceIdType.MESH
HIGHEST = lax.Precision.HIGHEST
WIDE = jnp.float32
NARROW = jnp.bfloat16


def remote(src, dst, sems, slot, device):
    return pltpu.make_async_remote_copy(
        src_ref=src, dst_ref=dst, send_sem=sems[0].at[slot], recv_sem=sems[1].at[slot],
        device_id=device, device_id_type=MESH,
    )


def meet(devices):
    barrier = pltpu.get_barrier_semaphore()
    for device in devices:
        pl.semaphore_signal(barrier, inc=1, device_id=device, device_id_type=MESH)
    pl.semaphore_wait(barrier, len(devices))


def gather_kernel(dims, left_ref, right_ref, cols_ref, xg, yg, yi, vg, send, recv, own):
    n_row, n_col, n_in, slots, js, width, cols = dims
    share = yi.shape[-1]
    row, col, inner = lax.axis_index("row"), lax.axis_index("col"), lax.axis_index("inner")
    twin_row = row + 1 - 2 * lax.rem(row, 2)
    far_row = lax.rem(row + 2, n_row)
    twin_far = lax.rem(twin_row + 2, n_row)
    sems = (send, recv)
    twin = {"row": twin_row}
    far = {"row": far_row}
    up = {"col": lax.rem(col + 1, n_col)}
    down = {"col": lax.rem(col + n_col - 1, n_col)}
    col_peers = [{"col": lax.rem(col + d, n_col)} for d in range(1, n_col)]
    inner_peers = [lax.rem(inner + d, n_in) for d in range(1, n_in)]
    meet([twin, far] + col_peers + [{"inner": p} for p in inner_peers])

    started = []

    def push(src, dst, device):
        copy = remote(src, dst, sems, len(started), device)
        copy.start()
        started.append(copy)
        return copy

    def place(k, r, c, part=None):
        first, length = (0, js) if part is None else (part * (js // 2), js // 2)
        return xg.at[
            k,
            pl.ds(pl.multiple_of(c * js + first, js // 2), length),
            pl.ds(pl.multiple_of(r * width, width), width),
        ]

    def y_place(r):
        return yg.at[:, :, pl.ds(pl.multiple_of(r * width, width), width)]

    def v_place(c):
        return vg.at[:, :, pl.ds(pl.multiple_of(c * cols, cols), cols)]

    half = n_col // 2
    y_far = push(right_ref, y_place(row), far)
    y_twin = push(right_ref, y_place(row), twin)
    v_copies = [push(cols_ref, v_place(col), peer) for peer in col_peers]
    far_got = []
    rings = {}
    twin_copies = []
    for k in range(slots):
        mine = left_ref.at[k]
        spot = place(k, row, col)
        far_got.append(push(mine, spot, far))
        rings[0, 1, k] = (push(mine, spot, up), push(mine, spot, down))
        twin_copies.append(push(mine, spot, twin))
    local_x = [pltpu.make_async_copy(left_ref.at[k], place(k, row, col), own.at[k]) for k in range(slots)]
    local_y = pltpu.make_async_copy(right_ref, y_place(row), own.at[slots])
    local_v = pltpu.make_async_copy(cols_ref, v_place(col), own.at[slots + 1])
    local_y.start()
    local_v.start()
    for copy in local_x:
        copy.start()
    y_far.wait_recv()
    y_twin_far = push(y_place(far_row), y_place(far_row), twin)
    rows = (row, far_row)
    for k in range(slots):
        far_got[k].wait_recv()
        spot = place(k, far_row, col)
        rings[1, 1, k] = (push(spot, spot, up), push(spot, spot, down))
        twin_copies.append(push(spot, spot, twin))
    local_y.wait()
    y_twin.wait_recv()
    y_twin_far.wait_recv()
    y_out = []
    for peer in inner_peers:
        src = yg.at[:, :, pl.ds(pl.multiple_of(peer * share, share), share)]
        y_out.append(push(src, yi.at[inner], {"inner": peer}))
    local_i = pltpu.make_async_copy(
        yg.at[:, :, pl.ds(pl.multiple_of(inner * share, share), share)], yi.at[inner], own.at[slots + 2]
    )
    local_i.start()
    for step in range(1, half + 1):
        for stream in range(2):
            for k in range(slots):
                got_up, got_down = rings[stream, step, k]
                from_up = lax.rem(col + n_col - step, n_col)
                from_down = lax.rem(col + step, n_col)
                parts = (None, None) if step < half else (0, 1)
                got_up.wait_recv()
                a = place(k, rows[stream], from_up, parts[0])
                if step < half:
                    last = step + 1 == half
                    a_next = place(k, rows[stream], from_up, 0) if last else a
                    next_up = push(a_next, a_next, up)
                twin_copies.append(push(a, a, twin))
                got_down.wait_recv()
                b = place(k, rows[stream], from_down, parts[1])
                if step < half:
                    b_next = place(k, rows[stream], from_down, 1) if last else b
                    next_down = push(b_next, b_next, down)
                    rings[stream, step + 1, k] = (next_up, next_down)
                twin_copies.append(push(b, b, twin))
    for copy in twin_copies + v_copies + y_out:
        copy.wait_recv()
    for copy in local_x + [local_v, local_i]:
        copy.wait()
    for copy in started:
        copy.wait_send()


def gather_all(left, right, cols_own, sizes):
    n_row, n_col, n_in = sizes
    slots, js, width = left.shape
    rank, cols = cols_own.shape[1:]
    total = width * n_row
    half = n_col // 2
    n_copies = 3 + (n_col - 1) + (n_in - 1) + slots * (4 + 3 + 2 * (2 * half + 2 * (half - 1)))
    dims = (n_row, n_col, n_in, slots, js, width, cols)
    any_spec = pl.BlockSpec(memory_space=pltpu.HBM)
    return pl.pallas_call(
        functools.partial(gather_kernel, dims),
        out_shape=(
            jax.ShapeDtypeStruct((slots, n_col * js, total), left.dtype),
            jax.ShapeDtypeStruct((slots, js, total), left.dtype),
            jax.ShapeDtypeStruct((n_in, slots, js, total // n_in), left.dtype),
            jax.ShapeDtypeStruct((slots, rank, total), left.dtype),
        ),
        in_specs=[any_spec] * 3,
        out_specs=[any_spec] * 4,
        scratch_shapes=[
            pltpu.SemaphoreType.DMA((n_copies,)),
            pltpu.SemaphoreType.DMA((n_copies,)),
            pltpu.SemaphoreType.DMA((slots + 3,)),
        ],
        compiler_params=pltpu.CompilerParams(collective_id=0, has_side_effects=True),
    )(left, right, cols_own)


def spread_kernel(dims, p_ref, z_ref, pr, zr, send, recv, zsend, zrecv, own):
    n_col, n_in, group = dims
    col, inner = lax.axis_index("col"), lax.axis_index("inner")
    home = lax.div(col, group)
    slot = lax.rem(col, group)
    meets = []
    targets = []
    for d in range(n_col):
        targets.append({"col": lax.rem(col + d, n_col), "inner": home})
    peers = [lax.rem(inner + d, n_in) for d in range(1, n_in)]
    barrier = pltpu.get_barrier_semaphore()
    n_all = 0
    for d in range(n_col):
        for e in range(n_in):
            if d or e:
                pl.semaphore_signal(
                    barrier, inc=1,
                    device_id={"col": lax.rem(col + d, n_col), "inner": lax.rem(inner + e, n_in)},
                    device_id_type=MESH,
                )
                n_all += 1
    pl.semaphore_wait(barrier, n_all)
    z_copies = []
    for e, peer in enumerate(peers):
        copy = remote(z_ref, zr.at[inner], (zsend, zrecv), e, {"inner": peer})
        copy.start()
        z_copies.append(copy)
    z_own = pltpu.make_async_copy(z_ref, zr.at[inner], own.at[1])
    z_own.start()

    def block(d):
        return pltpu.make_async_remote_copy(
            src_ref=p_ref.at[lax.rem(col + d, n_col)], dst_ref=pr.at[inner, slot],
            send_sem=send.at[d], recv_sem=recv.at[inner, slot],
            device_id=targets[d], device_id_type=MESH,
        )

    for d in range(1, n_col):
        block(d).start()

    @pl.when(home != inner)
    def _():
        block(0).start()

    @pl.when(home == inner)
    def _():
        pltpu.make_async_copy(p_ref.at[col], pr.at[inner, slot], own.at[0]).start()

    for e in range(n_in):
        for g in range(group):
            is_own = jnp.logical_and(inner == e, col == inner * group + g)

            @pl.when(jnp.logical_not(is_own))
            def _(e=e, g=g):
                pltpu.make_async_remote_copy(
                    src_ref=p_ref.at[0], dst_ref=pr.at[e, g], send_sem=send.at[0], recv_sem=recv.at[e, g],
                    device_id=targets[1], device_id_type=MESH,
                ).wait_recv()

    @pl.when(home == inner)
    def _():
        pltpu.make_async_copy(p_ref.at[col], pr.at[inner, slot], own.at[0]).wait()

    @pl.when(home != inner)
    def _():
        block(0).wait_send()

    for d in range(1, n_col):
        block(d).wait_send()
    z_own.wait()
    for copy in z_copies:
        copy.wait()


def spread(p, z, sizes):
    n_row, n_col, n_in = sizes
    group = n_col // n_in
    vmem = pl.BlockSpec(memory_space=pltpu.VMEM)
    return pl.pallas_call(
        functools.partial(spread_kernel, (n_col, n_in, group)),
        out_shape=(
            jax.ShapeDtypeStruct((n_in, group) + p.shape[1:], p.dtype),
            jax.ShapeDtypeStruct((n_in,) + z.shape, z.dtype),
        ),
        in_specs=[vmem, vmem],
        out_specs=[vmem, vmem],
        scratch_shapes=[
            pltpu.SemaphoreType.DMA((n_col,)),
            pltpu.SemaphoreType.DMA((n_in, group)),
            pltpu.SemaphoreType.DMA((n_in,)),
            pltpu.SemaphoreType.DMA((n_in,)),
            pltpu.SemaphoreType.DMA((2,)),
        ],
        compiler_params=pltpu.CompilerParams(collective_id=1, has_side_effects=True),
    )(p, z)


def total_kernel(n_in, part_ref, out_ref, got, send, recv):
    inner = lax.axis_index("inner")
    peers = [lax.rem(inner + d, n_in) for d in range(1, n_in)]
    meet([{"inner": peer} for peer in peers])
    copies = []
    for e, peer in enumerate(peers):
        copy = remote(part_ref, got.at[e], (send, recv), e, {"inner": peer})
        copy.start()
        copies.append(copy)
    for copy in copies:
        copy.wait()
    out = part_ref[...]
    for e in range(n_in - 1):
        out = out + got[e]
    out_ref[...] = out


def total_over_inner(part, n_in):
    vmem = pl.BlockSpec(memory_space=pltpu.VMEM)
    return pl.pallas_call(
        functools.partial(total_kernel, n_in),
        out_shape=jax.ShapeDtypeStruct(part.shape, part.dtype),
        in_specs=[vmem],
        out_specs=vmem,
        scratch_shapes=[
            pltpu.VMEM((n_in - 1,) + part.shape, part.dtype),
            pltpu.SemaphoreType.DMA((n_in - 1,)),
            pltpu.SemaphoreType.DMA((n_in - 1,)),
        ],
        compiler_params=pltpu.CompilerParams(collective_id=2, has_side_effects=True),
    )(part)


def inverse_factor_kernel(g_ref, out_ref):
    count, size, _ = g_ref.shape
    tall = lax.broadcasted_iota(jnp.int32, (size, size), 0)
    wide = lax.broadcasted_iota(jnp.int32, (size, size), 1)
    eye = (tall == wide).astype(WIDE)
    lines = lax.broadcasted_iota(jnp.int32, (8, 1), 0)
    works = []
    for j in range(count):
        full = jnp.concatenate([g_ref[j], eye], axis=1)
        works.append([full[8 * b : 8 * b + 8] for b in range(size // 8)])
    scales = [[] for _ in range(count)]
    for k in range(size):
        b0, in_b = k // 8, k % 8
        for j in range(count):
            work = works[j]
            line = work[b0][in_b : in_b + 1]
            pivot = line[:, k : k + 1]
            scales[j].append(lax.rsqrt(pivot))
            line = line * (1.0 / pivot)
            for b in range(b0, size // 8):
                column = work[b][:, k : k + 1]
                if b == b0:
                    if in_b == 7:
                        continue
                    column = jnp.where(lines > in_b, column, 0.0)
                work[b] = work[b] - column * line
    for j in range(count):
        scale = jnp.concatenate(scales[j], axis=0)
        out_ref[j] = jnp.concatenate(works[j], axis=0)[:, size:] * scale


def inverse_factor(gram):
    vmem = pl.BlockSpec(memory_space=pltpu.VMEM)
    return pl.pallas_call(
        inverse_factor_kernel,
        out_shape=jax.ShapeDtypeStruct(gram.shape, gram.dtype),
        in_specs=[vmem],
        out_specs=vmem,
    )(gram)


def local(sizes, near_flags, row_factor, col_factor, near_block, inner_left, inner_right, sketch_matrix):
    n_row, n_col, n_in = sizes
    slots, own_j, rank, width = inner_left.shape
    js = own_j * rank
    total = width * n_row
    cols = total // n_col
    share = total // n_in
    xg, yg, yi, vg = gather_all(
        inner_left.reshape(slots, js, width), inner_right.reshape(slots, js, width), col_factor[0], sizes
    )
    nearness = near_flags[0]
    pieces = []
    for slot in range(slots):

        def lowrank(slot=slot):
            coupled = lax.dot_general(
                xg[slot], vg[slot], (((1,), (1,)), ((), ())), preferred_element_type=WIDE
            ).astype(NARROW)
            return jnp.dot(coupled, row_factor[0, slot], preferred_element_type=WIDE).astype(NARROW)

        def neardense(slot=slot):
            return jnp.dot(xg[slot], near_block[0, slot], preferred_element_type=WIDE).astype(NARROW)

        pieces.append(lax.cond(nearness[slot] > 0, neardense, lowrank))
    spread_out = jnp.stack([p.reshape(n_col, js, cols) for p in pieces], axis=1)
    reduced = jnp.einsum(
        "kjrl,jsl->krjs", yg.reshape(slots, own_j, rank, total), sketch_matrix, preferred_element_type=WIDE
    ).astype(NARROW)
    got, reduced_all = spread(spread_out, reduced.reshape(slots * rank, js), sizes)
    group = n_col // n_in
    stacked = got.reshape(n_in, group, slots, own_j, rank, cols).transpose(3, 0, 2, 4, 1, 5)
    stacked = stacked.reshape(own_j, n_in * slots * rank, share)
    z_all = reduced_all.reshape(n_in * slots * rank, own_j, rank)
    sampled = jnp.einsum("ajs,jal->jsl", z_all, stacked, preferred_element_type=WIDE)
    high = sampled.astype(NARROW)
    low = (sampled - high.astype(WIDE)).astype(NARROW)
    both = jnp.concatenate([high, low], axis=1)
    cross = jnp.einsum("jsl,jal->jsa", both, stacked, preferred_element_type=WIDE)
    cross = cross[:, :rank] + cross[:, rank:]
    gram = jnp.einsum("jsl,jtl->jst", sampled, sampled, precision=HIGHEST) / total
    summed = total_over_inner(jnp.concatenate([cross, gram], axis=2), n_in)
    depth = n_in * slots * rank
    inverse = inverse_factor(summed[:, :, depth:])
    basis = jnp.einsum("jst,jtl->jsl", inverse, sampled, precision=HIGHEST)
    projected = jnp.einsum("jst,jta->jsa", inverse, summed[:, :, :depth], precision=HIGHEST) / math.sqrt(total)
    p_high = projected.astype(NARROW)
    p_low = (projected - p_high.astype(WIDE)).astype(NARROW)
    yk = yi.reshape(n_in * slots, own_j, rank, share)
    p_both = jnp.concatenate([p_high, p_low], axis=1).reshape(own_j, 2 * rank, n_in * slots, rank)
    coupling = jnp.einsum("jskr,kjrl->jsl", p_both, yk, preferred_element_type=WIDE)
    coupling = coupling[:, :rank] + coupling[:, rank:]
    return (basis[None], coupling[None])


def solution(mesh):
    sizes = (mesh.shape["row"], mesh.shape["col"], mesh.shape["inner"])
    in_specs = (
        P("row", "inner"),
        P("row", "inner", None, "col"),
        P("row", "inner", None, "col"),
        P("row", "inner", None, "col"),
        P("inner", "col", None, "row"),
        P("inner", "col", None, "row"),
        P("col", None, None),
    )
    out_specs = (P("row", "col", None, "inner"), P("row", "col", None, "inner"))
    return jax.shard_map(
        functools.partial(local, sizes), mesh=mesh, in_specs=in_specs, out_specs=out_specs, check_vma=False
    )
```

time: 535 us -> 279 us (0.52)
  waiting for transfers between devices: 388 us -> 0 us
  Pallas kernels: 0 us -> 223 us
  other arithmetic: 46.7 us -> 5.28 us
  blocking collectives: 25.4 us -> 0 us
  between operations: 15.9 us -> 2.72 us
  starting transfers between devices: 6.7 us -> 0 us
    all_gather x3 -> x0, waiting for transfers between devices: 226 us -> none  [the longest x1 195 us: local(): left_all = lax.all_gather(left_full, 'col', axis=1, tiled=True)]
    pallas_call x0 -> x4, Pallas kernels: none -> 223 us  [the longest x1 121 us: gather_all(): pl.pallas_call(functools.partial(gather_kernel, dims), out_shape=(jax.Sha...]
    all_to_all x1 -> x0, waiting for transfers between devices: 67.9 us -> none  [local(): lax.all_to_all(jnp.stack(pieces), 'col', split_axis=1, concat_axis=3, til...]
    psum x1 -> x0, waiting for transfers between devices: 64 us -> none  [local(): sampled = lax.psum(sampled_part, 'inner')]
    another operation x8 -> x1, other arithmetic: 46.7 us -> 3.24 us  [local(): spread_out = jnp.stack([p.reshape(n_col, js, cols) for p in pieces], axis=1)]
    reduce_scatter x1 -> x0, waiting for transfers between devices: 29.7 us -> none  [local(): lax.psum_scatter(coupling_part, 'inner', scatter_dimension=2, tiled=True)]
    all_gather x1 -> x0, blocking collectives: 25.4 us -> none  [local(): cols_full = lax.all_gather(col_factor[0], 'col', axis=2, tiled=True)]
    all_to_all x2 -> x0, local copies, waits for them, and re-layouts: 12.2 us -> none  [local(): lax.all_to_all(jnp.stack(pieces), 'col', split_axis=1, concat_axis=3, til...]
  transfers between devices with their start and end apart: 6 -> 0, of which waited for: 5 -> 0; matrix products, arithmetic and copies ran while one was open for 2% -> 0% of each run, Pallas kernels for 0% -> 0%
where the time goes in v1:
time: 279 us; the launch traced here: 277 us
  Pallas kernels  223 us (80%)
  matrix products  28.1 us (10%)
  local copies, waits for them, and re-layouts  17.6 us (6%)
  other arithmetic  5.28 us (2%)
    pallas_call x1, Pallas kernels, gather_all(): pl.pallas_call(functools.partial(gather_kernel, dims), out_shape=(jax.Sha...  121 us
    pallas_call x1, Pallas kernels, spread(): pl.pallas_call(functools.partial(spread_kernel, (n_col, n_in, group)), ou...  78.1 us
    pallas_call x1, Pallas kernels, total_over_inner(): pl.pallas_call(functools.partial(total_kernel, n_in), out_shape=jax.Shape...  16.3 us
    dot_general x3, matrix products, lowrank(): jnp.dot(coupled, row_factor[0, slot], preferred_element_type=WIDE)  13.3 us
    pallas_call x1, Pallas kernels, inverse_factor(): pl.pallas_call(inverse_factor_kernel, out_shape=jax.ShapeDtypeStruct(gram...  7.45 us
    transpose x1, local copies, waits for them, and re-layouts, local(): got.reshape(n_in, group, slots, own_j, rank, cols)  6.83 us
    reshape x1, local copies, waits for them, and re-layouts, local(): stacked = stacked.reshape(own_j, n_in * slots * rank, share)  6.12 us

profile of v1, /device:TPU:24, one launch (start us, length us, event | category | flops | bytes accessed | tf_op | source)
XLA Modules:
  0.0 277.0 jit_solution(1981874209076824725)
XLA Ops:
  0.6 1.4 fusion.93
  4.0 121.4 %shard_map.86 = (bf16[3,1024,2048]{2,1,0:T(8,128)(2,1)}, bf16[3,256,2048]{2,1,0:T(8,128)(2,1)}, bf16[2,3,256,1024]{3,2,1,0:T(8,128)(2,1)}, bf16[3,64,2048]{2,1,0:T(8,128)(2,1)}) custom-call(bf16[3,256,512]{2,1,0:T(8,128)(2,1)} %bitcast.130, bf16[3,256,512]{2,1,0:T(8,128)(2,1)} %bitcast.131, bf16[3,64,512]{2,1,0:T(8,128)(2,1)} %bitcast.132), custom_call_target="tpu_custom_call" | custom-call | tf_op jit(solution)/shard_map/pallas_call | solution.py:146
  125.4 2.9 %fusion.82 = bf16[3,64,4,64]{3,1,0,2:T(8,128)(2,1)S(1)} fusion(bf16[3,4,64,2048]{3,2,1,0:T(8,128)(2,1)} %bitcast.133, bf16[4,64,2048]{2,1,0:T(8,128)(2,1)S(1)} %copy-done), kind=kOutput, calls=%fused_computation.54 | convolution fusion | flops 201375744 | bytes 4292608 | tf_op jit(solution)/shard_map/kjrl,jsl->krjs/dot_general | solution.py:361
  129.3 4.1 %conditional.5 = (bf16[4,1,256,512]{3,2,0,1:T(8,128)(2,1)S(1)}) conditional(s32[]{:T(128)} %bitcast.28, (bf16[3,1024,2048]{2,1,0:T(8,128)(2,1)}, bf16[3,64,2048]{2,1,0:T(8,128)(2,1)}, bf16[1,3,64,512]{3,2,1,0:T(8,128)(2,1)S(1)}) %tuple.46, (bf16[3,1024,2048]{2,1,0:T(8,128)(2,1)}, bf16[1,3,2048,512]{3,2,1,0:T(8,128)(2,1)}) %tuple.33), branch_computations={%region_4.0_spmd, %region_5.0_spmd} | conditional | flops 2148007936 | bytes 7340040 | solution.py:359
  129.3 4.1 %convolution_convert_fusion.2 = bf16[1024,512]{1,0:T(8,128)(2,1)S(1)} fusion(bf16[3,1024,2048]{2,1,0:T(8,128)(2,1)} %get-tuple-element.52, bf16[3,64,2048]{2,1,0:T(8,128)(2,1)} %get-tuple-element.53, bf16[1,3,64,512]{3,2,1,0:T(8,128)(2,1)S(1)} %get-tuple-element.54), kind=kOutput, calls=%fused_computation.33 | convolution fusion | flops 336134144 | bytes 5570560 | tf_op jit(solution)/shard_map/cond/branch_0_fun/dot_general | solution.py:354
  133.4 4.1 %conditional.4 = (bf16[4,1,256,512]{3,2,0,1:T(8,128)(2,1)S(1)}) conditional(s32[]{:T(128)} %bitcast.26, (bf16[3,1024,2048]{2,1,0:T(8,128)(2,1)}, bf16[3,64,2048]{2,1,0:T(8,128)(2,1)}, bf16[1,3,64,512]{3,2,1,0:T(8,128)(2,1)S(1)}) %tuple.47, (bf16[3,1024,2048]{2,1,0:T(8,128)(2,1)}, bf16[1,3,2048,512]{3,2,1,0:T(8,128)(2,1)}) %tuple.33), branch_computations={%region_2.0_spmd, %region_3.0_spmd} | conditional | flops 2148007936 | bytes 7340040 | solution.py:359
  133.4 4.1 %convolution_convert_fusion.1 = bf16[1024,512]{1,0:T(8,128)(2,1)S(1)} fusion(bf16[3,1024,2048]{2,1,0:T(8,128)(2,1)} %get-tuple-element.47, bf16[3,64,2048]{2,1,0:T(8,128)(2,1)} %get-tuple-element.48, bf16[1,3,64,512]{3,2,1,0:T(8,128)(2,1)S(1)} %get-tuple-element.49), kind=kOutput, calls=%fused_computation.18 | convolution fusion | flops 336134144 | bytes 5570560 | tf_op jit(solution)/shard_map/cond/branch_0_fun/dot_general | solution.py:354
  137.5 5.1 %conditional.3 = (bf16[4,1,256,512]{3,2,0,1:T(8,128)(2,1)}) conditional(s32[]{:T(128)} %bitcast.21, (bf16[3,1024,2048]{2,1,0:T(8,128)(2,1)}, bf16[3,64,2048]{2,1,0:T(8,128)(2,1)}, bf16[1,3,64,512]{3,2,1,0:T(8,128)(2,1)S(1)}) %tuple.48, (bf16[3,1024,2048]{2,1,0:T(8,128)(2,1)}, bf16[1,3,2048,512]{3,2,1,0:T(8,128)(2,1)}) %tuple.33), branch_computations={%region_0.0_spmd, %region_1.0_spmd} | conditional | flops 2148007936 | bytes 7340040 | solution.py:359
  137.5 5.1 %convolution_convert_fusion = bf16[1024,512]{1,0:T(8,128)(2,1)} fusion(bf16[3,1024,2048]{2,1,0:T(8,128)(2,1)} %get-tuple-element.42, bf16[3,64,2048]{2,1,0:T(8,128)(2,1)} %get-tuple-element.43, bf16[1,3,64,512]{3,2,1,0:T(8,128)(2,1)S(1)} %get-tuple-element.44), kind=kOutput, calls=%fused_computation.3 | convolution fusion | flops 336134144 | bytes 5570560 | tf_op jit(solution)/shard_map/cond/branch_0_fun/dot_general | solution.py:354
  142.6 3.2 %pad_maximum_fusion.p_ref = bf16[4,3,256,512]{3,2,1,0:T(8,128)(2,1)} fusion(bf16[4,1,256,512]{3,2,1,0:T(8,128)(2,1)S(1)} %bitcast.123, bf16[4,1,256,512]{3,2,1,0:T(8,128)(2,1)S(1)} %bitcast.126, bf16[4,1,256,512]{3,2,1,0:T(8,128)(2,1)} %bitcast.129), kind=kLoop, calls=%fused_computation.45 | loop fusion | flops 3145728 | bytes 6291456 | tf_op jit(solution)/shard_map/stack | solution.py:360
  145.9 78.1 %shard_map.87 = (bf16[2,2,3,256,512]{4,3,2,1,0:T(8,128)(2,1)}, bf16[2,192,256]{2,1,0:T(8,128)(2,1)}) custom-call(bf16[4,3,256,512]{3,2,1,0:T(8,128)(2,1)} %pad_maximum_fusion.p_ref, bf16[192,256]{1,0:T(8,128)(2,1)} %reshape.52.z_ref), custom_call_target="tpu_custom_call" | custom-call | tf_op jit(solution)/shard_map/pallas_call | solution.py:243
  224.0 6.8 %copy.24 = bf16[4,2,3,64,2,512]{5,4,3,2,1,0:T(2,128)(2,1)} copy(bf16[4,2,3,64,2,512]{5,3,0,2,4,1:T(8,128)(2,1)} %bitcast.119) | data formatting | bytes 6291456 | tf_op jit(solution)/shard_map/transpose | solution.py:366
  230.8 6.1 %reshape.55 = bf16[4,384,1024]{2,1,0:T(8,128)(2,1)} reshape(bf16[4,2,3,64,2,512]{5,4,3,2,1,0:T(2,128)(2,1)} %copy.24) | data formatting | bytes 6291456 | tf_op jit(solution)/shard_map/reshape | solution.py:367
  237.3 2.7 subtract_convert_fusion
  240.1 1.1 fusion.86
  241.3 1.1 convolution_multiply_fusion.1
  242.4 0.8 pad_maximum_fusion.1.part_ref
  243.2 16.3 %shard_map.88 = f32[4,64,448]{2,1,0:T(8,128)} custom-call(f32[4,64,448]{2,1,0:T(8,128)} %pad_maximum_fusion.1.part_ref), custom_call_target="tpu_custom_call" | custom-call | tf_op jit(solution)/shard_map/pallas_call | solution.py:281
  259.5 1.6 slice.80.g_ref
  261.1 7.5 %shard_map.89 = f32[4,64,64]{2,1,0:T(8,128)} custom-call(f32[4,64,64]{2,1,0:T(8,128)} %slice.80.g_ref), custom_call_target="tpu_custom_call" | custom-call | tf_op jit(solution)/shard_map/pallas_call | solution.py:328
  268.5 1.5 subtract_convert_fusion.1
  270.1 2.9 %convolution_bitcast_fusion = f32[1,4,64,1024]{3,2,1,0:T(8,128)} fusion(f32[4,64,64]{2,1,0:T(8,128)} %shard_map.89, f32[4,64,1024]{2,1,0:T(8,128)S(1)} %get-tuple-element.78), kind=kOutput, calls=%fused_computation.51 | convolution fusion | flops 201326592 | bytes 2162688 | tf_op jit(solution)/shard_map/jst,jtl->jsl/dot_general | solution.py:379
  273.2 2.7 fusion.76
  275.9 1.1 fusion.85
  (15 shorter events, 1.7 us)
Async XLA Ops:
  0.6 124.7 %copy-start = (bf16[4,64,2048]{2,1,0:T(8,128)(2,1)S(1)}, bf16[4,64,2048]{2,1,0:T(8,128)(2,1)}, u32[]{:S(2)}) copy-start(bf16[4,64,2048]{2,1,0:T(8,128)(2,1)} %param.19) | copy-start | bytes 3145732
  125.4 3.9 %copy-start.3 = (bf16[1,3,64,512]{3,2,1,0:T(8,128)(2,1)S(1)}, bf16[1,3,64,512]{3,2,1,0:T(8,128)(2,1)}, u32[]{:S(2)}) copy-start(bf16[1,3,64,512]{3,2,1,0:T(8,128)(2,1)} %param.14) | copy-start | bytes 589828
  230.8 6.1 %copy-start.2 = (bf16[2,192,256]{2,1,0:T(8,128)(2,1)S(1)}, bf16[2,192,256]{2,1,0:T(8,128)(2,1)}, u32[]{:S(2)}) copy-start(bf16[2,192,256]{2,1,0:T(8,128)(2,1)} %get-tuple-element.68) | copy-start | bytes 589828
  237.3 2.8 %copy-start.1 = (bf16[4,384,1024]{2,1,0:T(8,128)(2,1)S(1)}, bf16[4,384,1024]{2,1,0:T(8,128)(2,1)}, u32[]{:S(2)}) copy-start(bf16[4,384,1024]{2,1,0:T(8,128)(2,1)} %reshape.55) | copy-start | bytes 9437188

commit v2 on v1

v2 whole, which is shorter than its diff:
```python
import functools
import math

import jax
import jax.numpy as jnp
from jax import lax
from jax.experimental import pallas as pl
from jax.experimental.pallas import tpu as pltpu
from jax.sharding import PartitionSpec as P

MESH = pl.DeviceIdType.MESH
HIGHEST = lax.Precision.HIGHEST
WIDE = jnp.float32
NARROW = jnp.bfloat16


def remote(src, dst, sems, slot, device):
    return pltpu.make_async_remote_copy(
        src_ref=src, dst_ref=dst, send_sem=sems[0].at[slot], recv_sem=sems[1].at[slot],
        device_id=device, device_id_type=MESH,
    )


def meet(devices):
    barrier = pltpu.get_barrier_semaphore()
    for device in devices:
        pl.semaphore_signal(barrier, inc=1, device_id=device, device_id_type=MESH)
    pl.semaphore_wait(barrier, len(devices))


def gather_kernel(dims, left_ref, right_ref, cols_ref, xg, yg, yi, vg, stage, send, recv, own):
    n_row, n_col, n_in, slots, js, width, rank, cols = dims
    share = yi.shape[-1]
    row, col, inner = lax.axis_index("row"), lax.axis_index("col"), lax.axis_index("inner")
    twin_row = row + 1 - 2 * lax.rem(row, 2)
    far_row = lax.rem(row + 2, n_row)
    sems = (send, recv)
    twin = {"row": twin_row}
    far = {"row": far_row}
    up = {"col": lax.rem(col + 1, n_col)}
    down = {"col": lax.rem(col + n_col - 1, n_col)}
    inner_peers = [lax.rem(inner + d, n_in) for d in range(1, n_in)]
    meet([twin, far, up, down] + [{"inner": p} for p in inner_peers])

    started = []

    def push(src, dst, device):
        copy = remote(src, dst, sems, len(started), device)
        copy.start()
        started.append(copy)
        return copy

    def x_place(r):
        def place(k, c, part=None):
            first, length = (0, js) if part is None else (part * (js // 2), js // 2)
            return xg.at[
                k,
                pl.ds(pl.multiple_of(c * js + first, js // 2), length),
                pl.ds(pl.multiple_of(r * width, width), width),
            ]

        return place

    def y_place(r):
        return yg.at[:, :, pl.ds(pl.multiple_of(r * width, width), width)]

    def v_place(k, c, part=None):
        rows = pl.ds(0, rank) if part is None else pl.ds(part * (rank // 2), rank // 2)
        return vg.at[:, rows, pl.ds(pl.multiple_of(c * cols, cols), cols)]

    half = n_col // 2
    twins = []

    def ring_start(src, place, k):
        spot = place(k, col)
        return (push(src, spot, up), push(src, spot, down))

    def ring_step(pair, place, k, step, relay):
        got_up, got_down = pair
        from_up = lax.rem(col + n_col - step, n_col)
        from_down = lax.rem(col + step, n_col)
        nexts = []
        for got, source, device, part in ((got_up, from_up, up, 0), (got_down, from_down, down, 1)):
            got.wait_recv()
            here = place(k, source, None if step < half else part)
            if step < half:
                on = place(k, source, part) if step + 1 == half else here
                nexts.append(push(on, on, device))
            if relay:
                twins.append(push(here, here, twin))
        return tuple(nexts)

    near, other = x_place(row), x_place(far_row)
    y_far = push(right_ref, y_place(row), far)
    near_rings, far_got = [], []
    for k in range(slots):
        near_rings.append(ring_start(left_ref.at[k], near, k))
        far_got.append(push(left_ref.at[k], near(k, col), far))
    v_ring = ring_start(cols_ref, v_place, 0)
    y_twin = push(right_ref, y_place(row), twin)
    for k in range(slots):
        twins.append(push(left_ref.at[k], near(k, col), twin))
    locals_ = [pltpu.make_async_copy(left_ref.at[k], near(k, col), own.at[k]) for k in range(slots)]
    local_y = pltpu.make_async_copy(right_ref, y_place(row), own.at[slots])
    locals_.append(pltpu.make_async_copy(cols_ref, v_place(0, col), own.at[slots + 1]))
    local_y.start()
    for copy in locals_:
        copy.start()
    for k in range(slots):
        near_rings[k] = ring_step(near_rings[k], near, k, 1, True)
    y_far.wait_recv()
    y_twin_far = push(y_place(far_row), y_place(far_row), twin)
    far_rings, y_out = [], []
    for k in range(slots):
        far_got[k].wait_recv()
        spot = other(k, col)
        far_rings.append(ring_start(spot, other, k))
        twins.append(push(spot, spot, twin))
        if k == 0:
            local_y.wait()
            y_twin.wait_recv()
            y_twin_far.wait_recv()
            for peer in inner_peers:
                src = yg.at[:, :, pl.ds(pl.multiple_of(peer * share, share), share)]
                y_out.append(push(src, yi.at[inner], {"inner": peer}))
            fetch = pltpu.make_async_copy(
                yg.at[:, :, pl.ds(pl.multiple_of(inner * share, share), share)], stage, own.at[slots + 2]
            )
            fetch.start()
    v_ring = ring_step(v_ring, v_place, 0, 1, False)
    fetch.wait()
    store = pltpu.make_async_copy(stage, yi.at[inner], own.at[slots + 3])
    store.start()
    for k in range(slots):
        far_rings[k] = ring_step(far_rings[k], other, k, 1, True)
    for step in range(2, half + 1):
        for k in range(slots):
            near_rings[k] = ring_step(near_rings[k], near, k, step, True)
        v_ring = ring_step(v_ring, v_place, 0, step, False)
        for k in range(slots):
            far_rings[k] = ring_step(far_rings[k], other, k, step, True)
    for copy in twins + y_out:
        copy.wait_recv()
    for copy in locals_ + [store]:
        copy.wait()
    for copy in started:
        copy.wait_send()


def gather_all(left, right, cols_own, sizes):
    n_row, n_col, n_in = sizes
    slots, js, width = left.shape
    rank, cols = cols_own.shape[1:]
    total = width * n_row
    half = n_col // 2
    n_copies = 3 + (n_in - 1) + slots * 3 + (2 * slots + 1) * 2 * half + 2 * slots * 2 * half
    dims = (n_row, n_col, n_in, slots, js, width, rank, cols)
    hbm = pl.BlockSpec(memory_space=pltpu.HBM)
    vmem = pl.BlockSpec(memory_space=pltpu.VMEM)
    return pl.pallas_call(
        functools.partial(gather_kernel, dims),
        out_shape=(
            jax.ShapeDtypeStruct((slots, n_col * js, total), left.dtype),
            jax.ShapeDtypeStruct((slots, js, total), left.dtype),
            jax.ShapeDtypeStruct((n_in, slots, js, total // n_in), left.dtype),
            jax.ShapeDtypeStruct((slots, rank, total), left.dtype),
        ),
        in_specs=[vmem] * 3,
        out_specs=[hbm] * 4,
        scratch_shapes=[
            pltpu.VMEM((slots, js, total // n_in), left.dtype),
            pltpu.SemaphoreType.DMA((n_copies,)),
            pltpu.SemaphoreType.DMA((n_copies,)),
            pltpu.SemaphoreType.DMA((slots + 4,)),
        ],
        compiler_params=pltpu.CompilerParams(collective_id=0, has_side_effects=True),
    )(left, right, cols_own)


def spread_kernel(dims, p_ref, z_ref, pr, zr, relay, send, recv, hop_send, hop_recv, on_send, on_recv, zsend, zrecv, own):
    n_col, n_in, group, own_j, cols = dims
    col, inner = lax.axis_index("col"), lax.axis_index("inner")
    half, half_j = n_col // 2, own_j // 2

    def home(c):
        return lax.div(c, group)

    def column(d):
        return lax.rem(col + n_col + d, n_col)

    def window(c, first=0, length=own_j):
        at = pl.multiple_of(lax.rem(c, group) * cols, cols)
        return pr.at[pl.ds(first, length), inner, :, :, pl.ds(at, cols)]

    meet([
        {"col": column(d), "inner": lax.rem(inner + e, n_in)}
        for d in range(n_col) for e in range(n_in) if d or e
    ])
    sides = (1, -1)
    hops = []
    for n, side in enumerate(sides):
        hop = remote(
            p_ref.at[column(half), pl.ds(n * half_j, half_j)], relay.at[n], (hop_send, hop_recv), n,
            {"col": column(side)},
        )
        hop.start()
        hops.append(hop)

    def block(d):
        return pltpu.make_async_remote_copy(
            src_ref=p_ref.at[column(d)], dst_ref=window(col),
            send_sem=send.at[d], recv_sem=recv.at[inner, lax.rem(col, group)],
            device_id={"col": column(d), "inner": home(col)}, device_id_type=MESH,
        )

    mine = pltpu.make_async_copy(p_ref.at[col], window(col), own.at[0])
    others = [d for d in range(1, n_col) if d != half]
    for d in others:
        block(d).start()

    @pl.when(home(col) != inner)
    def _():
        block(0).start()

    @pl.when(home(col) == inner)
    def _():
        mine.start()

    z_copies = []
    for e in range(1, n_in):
        copy = remote(z_ref, zr.at[inner], (zsend, zrecv), e - 1, {"inner": lax.rem(inner + e, n_in)})
        copy.start()
        z_copies.append(copy)
    z_own = pltpu.make_async_copy(z_ref, zr.at[inner], own.at[1])
    z_own.start()

    ons = []
    for n, side in enumerate(sides):
        hops[n].wait_recv()
        source = column(-side)
        on = pltpu.make_async_remote_copy(
            src_ref=relay.at[n], dst_ref=window(source, n * half_j, half_j),
            send_sem=on_send.at[n], recv_sem=on_recv.at[n, inner],
            device_id={"col": column(half - side), "inner": home(source)}, device_id_type=MESH,
        )
        on.start()
        ons.append(on)

    for e in range(n_in):
        for g in range(group):
            source = inner * group + g
            tied = source == column(half)
            is_own = jnp.logical_and(inner == e, col == source)

            @pl.when(tied)
            def _(e=e):
                for n in range(2):
                    pltpu.make_async_remote_copy(
                        src_ref=relay.at[n], dst_ref=relay.at[n],
                        send_sem=on_send.at[n], recv_sem=on_recv.at[n, e],
                        device_id={"col": column(1), "inner": inner}, device_id_type=MESH,
                    ).wait_recv()

            @pl.when(jnp.logical_not(jnp.logical_or(tied, is_own)))
            def _(e=e, g=g):
                pltpu.make_async_remote_copy(
                    src_ref=p_ref.at[0], dst_ref=p_ref.at[0], send_sem=send.at[0], recv_sem=recv.at[e, g],
                    device_id={"col": column(1), "inner": inner}, device_id_type=MESH,
                ).wait_recv()

    @pl.when(home(col) == inner)
    def _():
        mine.wait()

    @pl.when(home(col) != inner)
    def _():
        block(0).wait_send()

    for d in others:
        block(d).wait_send()
    for copy in hops + ons:
        copy.wait_send()
    z_own.wait()
    for copy in z_copies:
        copy.wait()


def spread(p, z, sizes):
    n_row, n_col, n_in = sizes
    group = n_col // n_in
    own_j, slots, rank, cols = p.shape[1:]
    vmem = pl.BlockSpec(memory_space=pltpu.VMEM)
    return pl.pallas_call(
        functools.partial(spread_kernel, (n_col, n_in, group, own_j, cols)),
        out_shape=(
            jax.ShapeDtypeStruct((own_j, n_in, slots, rank, group * cols), p.dtype),
            jax.ShapeDtypeStruct((n_in,) + z.shape, z.dtype),
        ),
        in_specs=[vmem, vmem],
        out_specs=[vmem, vmem],
        scratch_shapes=[
            pltpu.VMEM((2, own_j // 2, slots, rank, cols), p.dtype),
            pltpu.SemaphoreType.DMA((n_col,)),
            pltpu.SemaphoreType.DMA((n_in, group)),
            pltpu.SemaphoreType.DMA((2,)),
            pltpu.SemaphoreType.DMA((2,)),
            pltpu.SemaphoreType.DMA((2,)),
            pltpu.SemaphoreType.DMA((2, n_in)),
            pltpu.SemaphoreType.DMA((n_in,)),
            pltpu.SemaphoreType.DMA((n_in,)),
            pltpu.SemaphoreType.DMA((2,)),
        ],
        compiler_params=pltpu.CompilerParams(collective_id=1, has_side_effects=True),
    )(p, z)


def factor_kernel(n_in, gram_ref, cross_ref, inv_ref, out_ref, gram_got, cross_got, send, recv, csend, crecv):
    inner = lax.axis_index("inner")
    peers = [lax.rem(inner + d, n_in) for d in range(1, n_in)]
    meet([{"inner": peer} for peer in peers])
    grams = [remote(gram_ref, gram_got.at[e], (send, recv), e, {"inner": p}) for e, p in enumerate(peers)]
    crosses = [remote(cross_ref, cross_got.at[e], (csend, crecv), e, {"inner": p}) for e, p in enumerate(peers)]
    for copy in grams + crosses:
        copy.start()
    for copy in grams:
        copy.wait()
    gram = gram_ref[...]
    for e in range(n_in - 1):
        gram = gram + gram_got[e]
    inverse_factor(gram, inv_ref)
    for copy in crosses:
        copy.wait()
    cross = cross_ref[...]
    for e in range(n_in - 1):
        cross = cross + cross_got[e]
    out_ref[...] = cross


def factor_over_inner(gram, cross, n_in):
    vmem = pl.BlockSpec(memory_space=pltpu.VMEM)
    return pl.pallas_call(
        functools.partial(factor_kernel, n_in),
        out_shape=(
            jax.ShapeDtypeStruct(gram.shape, gram.dtype),
            jax.ShapeDtypeStruct(cross.shape, cross.dtype),
        ),
        in_specs=[vmem, vmem],
        out_specs=[vmem, vmem],
        scratch_shapes=[
            pltpu.VMEM((n_in - 1,) + gram.shape, gram.dtype),
            pltpu.VMEM((n_in - 1,) + cross.shape, cross.dtype),
        ] + [pltpu.SemaphoreType.DMA((n_in - 1,))] * 4,
        compiler_params=pltpu.CompilerParams(collective_id=2, has_side_effects=True),
    )(gram, cross)


def inverse_factor(gram, out_ref):
    count, size, _ = gram.shape
    tall = lax.broadcasted_iota(jnp.int32, (size, size), 0)
    wide = lax.broadcasted_iota(jnp.int32, (size, size), 1)
    eye = (tall == wide).astype(WIDE)
    lines = lax.broadcasted_iota(jnp.int32, (8, 1), 0)
    works = []
    for j in range(count):
        full = jnp.concatenate([gram[j], eye], axis=1)
        works.append([full[8 * b : 8 * b + 8] for b in range(size // 8)])
    scales = [[] for _ in range(count)]
    for k in range(size):
        b0, in_b = k // 8, k % 8
        for j in range(count):
            work = works[j]
            line = work[b0][in_b : in_b + 1]
            pivot = line[:, k : k + 1]
            scales[j].append(lax.rsqrt(pivot))
            line = line * (1.0 / pivot)
            for b in range(b0, size // 8):
                column = work[b][:, k : k + 1]
                if b == b0:
                    if in_b == 7:
                        continue
                    column = jnp.where(lines > in_b, column, 0.0)
                work[b] = work[b] - column * line
    for j in range(count):
        scale = jnp.concatenate(scales[j], axis=0)
        out_ref[j] = jnp.concatenate(works[j], axis=0)[:, size:] * scale


def local(sizes, near_flags, row_factor, col_factor, near_block, inner_left, inner_right, sketch_matrix):
    n_row, n_col, n_in = sizes
    slots, own_j, rank, width = inner_left.shape
    js = own_j * rank
    total = width * n_row
    cols = total // n_col
    share = total // n_in
    xg, yg, yi, vg = gather_all(
        inner_left.reshape(slots, js, width), inner_right.reshape(slots, js, width), col_factor[0], sizes
    )
    nearness = near_flags[0]
    pieces = []
    for slot in range(slots):

        def lowrank(slot=slot):
            coupled = lax.dot_general(
                xg[slot], vg[slot], (((1,), (1,)), ((), ())), preferred_element_type=WIDE
            ).astype(NARROW)
            return jnp.dot(coupled, row_factor[0, slot], preferred_element_type=WIDE).astype(NARROW)

        def neardense(slot=slot):
            return jnp.dot(xg[slot], near_block[0, slot], preferred_element_type=WIDE).astype(NARROW)

        pieces.append(lax.cond(nearness[slot] > 0, neardense, lowrank))
    spread_out = jnp.stack([p.reshape(n_col, own_j, rank, cols) for p in pieces], axis=2)
    reduced = jnp.einsum(
        "kjrl,jsl->krjs", yg.reshape(slots, own_j, rank, total), sketch_matrix, preferred_element_type=WIDE
    ).astype(NARROW)
    got, reduced_all = spread(spread_out, reduced.reshape(slots * rank, js), sizes)
    stacked = got.reshape(own_j, n_in * slots * rank, share)
    z_all = reduced_all.reshape(n_in * slots * rank, own_j, rank)
    sampled = jnp.einsum("ajs,jal->jsl", z_all, stacked, preferred_element_type=WIDE)
    high = sampled.astype(NARROW)
    low = (sampled - high.astype(WIDE)).astype(NARROW)
    both = jnp.concatenate([high, low], axis=1)
    cross = jnp.einsum("jsl,jal->jsa", both, stacked, preferred_element_type=WIDE)
    cross = cross[:, :rank] + cross[:, rank:]
    gram = jnp.einsum("jsl,jtl->jst", sampled, sampled, precision=HIGHEST) / total
    inverse, cross = factor_over_inner(gram, cross, n_in)
    basis = jnp.einsum("jst,jtl->jsl", inverse, sampled, precision=HIGHEST)
    projected = jnp.einsum("jst,jta->jsa", inverse, cross, precision=HIGHEST) / math.sqrt(total)
    p_high = projected.astype(NARROW)
    p_low = (projected - p_high.astype(WIDE)).astype(NARROW)
    yk = yi.reshape(n_in * slots, own_j, rank, share)
    p_both = jnp.concatenate([p_high, p_low], axis=1).reshape(own_j, 2 * rank, n_in * slots, rank)
    coupling = jnp.einsum("jskr,kjrl->jsl", p_both, yk, preferred_element_type=WIDE)
    coupling = coupling[:, :rank] + coupling[:, rank:]
    return (basis[None], coupling[None])


def solution(mesh):
    sizes = (mesh.shape["row"], mesh.shape["col"], mesh.shape["inner"])
    in_specs = (
        P("row", "inner"),
        P("row", "inner", None, "col"),
        P("row", "inner", None, "col"),
        P("row", "inner", None, "col"),
        P("inner", "col", None, "row"),
        P("inner", "col", None, "row"),
        P("col", None, None),
    )
    out_specs = (P("row", "col", None, "inner"), P("row", "col", None, "inner"))
    return jax.shard_map(
        functools.partial(local, sizes), mesh=mesh, in_specs=in_specs, out_specs=out_specs, check_vma=False
    )
```

time: 279 us -> 259 us (0.928)
  local copies, waits for them, and re-layouts: 17.6 us -> 4.01 us
  Pallas kernels: 223 us -> 215 us
  matrix products: 28.1 us -> 30.9 us
    dot_general x1 -> x3, matrix products: 1.54 us -> 11.9 us  [the longest x2 10.4 us: neardense(): jnp.dot(xg[slot], near_block[0, slot], preferred_element_type=WIDE)]
    pallas_call x3 -> x2, Pallas kernels: 102 us -> 92.6 us  [the longest x1 77.2 us: spread(): pl.pallas_call(functools.partial(spread_kernel, (n_col, n_in, group, own_...]
    dot_general x3 -> x1, matrix products: 13.3 us -> 5.08 us  [lowrank(): jnp.dot(coupled, row_factor[0, slot], preferred_element_type=WIDE)]
    transpose x1 -> x0, local copies, waits for them, and re-layouts: 6.83 us -> none  [local(): got.reshape(n_in, group, slots, own_j, rank, cols)]
    reshape x1 -> x0, local copies, waits for them, and re-layouts: 6.12 us -> none  [local(): stacked = stacked.reshape(own_j, n_in * slots * rank, share)]
where the time goes in v2:
time: 259 us; the launch traced here: 258 us
  Pallas kernels  215 us (83%)
  matrix products  30.9 us (12%)
  other arithmetic  5.14 us (2%)
  local copies, waits for them, and re-layouts  4.01 us (2%)
  between operations  2.7 us (1%)
    pallas_call x1, Pallas kernels, gather_all(): pl.pallas_call(functools.partial(gather_kernel, dims), out_shape=(jax.Sha...  122 us
    pallas_call x1, Pallas kernels, spread(): pl.pallas_call(functools.partial(spread_kernel, (n_col, n_in, group, own_...  77.2 us
    pallas_call x1, Pallas kernels, factor_over_inner(): pl.pallas_call(functools.partial(factor_kernel, n_in), out_shape=(jax.Sha...  15.4 us
    dot_general x2, matrix products, neardense(): jnp.dot(xg[slot], near_block[0, slot], preferred_element_type=WIDE)  10.4 us

profile of v2, /device:TPU:24, one launch (start us, length us, event | category | flops | bytes accessed | tf_op | source)
XLA Modules:
  0.0 257.8 jit_solution(200051847825452977)
XLA Ops:
  0.6 1.4 fusion.92
  4.0 122.4 %shard_map.86 = (bf16[3,1024,2048]{2,1,0:T(8,128)(2,1)}, bf16[3,256,2048]{2,1,0:T(8,128)(2,1)}, bf16[2,3,256,1024]{3,2,1,0:T(8,128)(2,1)}, bf16[3,64,2048]{2,1,0:T(8,128)(2,1)}) custom-call(bf16[3,256,512]{2,1,0:T(8,128)(2,1)} %bitcast.130, bf16[3,256,512]{2,1,0:T(8,128)(2,1)} %bitcast.131, bf16[3,64,512]{2,1,0:T(8,128)(2,1)} %bitcast.132), custom_call_target="tpu_custom_call" | custom-call | tf_op jit(solution)/shard_map/pallas_call | solution.py:160
  126.4 2.9 %fusion.82 = bf16[3,64,4,64]{3,1,0,2:T(8,128)(2,1)S(1)} fusion(bf16[3,4,64,2048]{3,2,1,0:T(8,128)(2,1)} %bitcast.133, bf16[4,64,2048]{2,1,0:T(8,128)(2,1)S(1)} %copy-done), kind=kOutput, calls=%fused_computation.54 | convolution fusion | flops 201375744 | bytes 4292608 | tf_op jit(solution)/shard_map/kjrl,jsl->krjs/dot_general | solution.py:413
  129.5 0.8 reshape.49.z_ref
  130.3 5.2 %conditional.5 = (bf16[4,4,1,64,512]{4,3,1,0,2:T(8,128)(2,1)S(1)}) conditional(s32[]{:T(128)} %bitcast.28, (bf16[3,1024,2048]{2,1,0:T(8,128)(2,1)}, bf16[3,64,2048]{2,1,0:T(8,128)(2,1)}, bf16[1,3,64,512]{3,2,1,0:T(8,128)(2,1)S(1)}) %tuple.46, (bf16[3,1024,2048]{2,1,0:T(8,128)(2,1)}, bf16[1,3,2048,512]{3,2,1,0:T(8,128)(2,1)}) %tuple.33), branch_computations={%region_4.0_spmd, %region_5.0_spmd} | conditional | flops 2148007936 | bytes 7340040 | solution.py:411
  130.3 5.2 %fusion.67 = bf16[1024,512]{1,0:T(8,128)(2,1)S(1)} fusion(bf16[1,3,2048,512]{3,2,1,0:T(8,128)(2,1)} %get-tuple-element.56, bf16[3,1024,2048]{2,1,0:T(8,128)(2,1)} %get-tuple-element.55), kind=kOutput, calls=%fused_computation.44 | convolution fusion | flops 2148007936 | bytes 7340032 | tf_op jit(solution)/shard_map/cond/branch_1_fun/dot_general | solution.py:409
  135.5 5.2 %conditional.4 = (bf16[4,4,1,64,512]{4,3,1,0,2:T(8,128)(2,1)S(1)}) conditional(s32[]{:T(128)} %bitcast.26, (bf16[3,1024,2048]{2,1,0:T(8,128)(2,1)}, bf16[3,64,2048]{2,1,0:T(8,128)(2,1)}, bf16[1,3,64,512]{3,2,1,0:T(8,128)(2,1)S(1)}) %tuple.47, (bf16[3,1024,2048]{2,1,0:T(8,128)(2,1)}, bf16[1,3,2048,512]{3,2,1,0:T(8,128)(2,1)}) %tuple.33), branch_computations={%region_2.0_spmd, %region_3.0_spmd} | conditional | flops 2148007936 | bytes 7340040 | solution.py:411
  135.5 5.2 %fusion.43 = bf16[1024,512]{1,0:T(8,128)(2,1)S(1)} fusion(bf16[1,3,2048,512]{3,2,1,0:T(8,128)(2,1)} %get-tuple-element.51, bf16[3,1024,2048]{2,1,0:T(8,128)(2,1)} %get-tuple-element.50), kind=kOutput, calls=%fused_computation.29 | convolution fusion | flops 2148007936 | bytes 7340032 | tf_op jit(solution)/shard_map/cond/branch_1_fun/dot_general | solution.py:409
  140.7 5.1 %conditional.3 = (bf16[4,4,1,64,512]{4,3,1,0,2:T(8,128)(2,1)}) conditional(s32[]{:T(128)} %bitcast.21, (bf16[3,1024,2048]{2,1,0:T(8,128)(2,1)}, bf16[3,64,2048]{2,1,0:T(8,128)(2,1)}, bf16[1,3,64,512]{3,2,1,0:T(8,128)(2,1)S(1)}) %tuple.48, (bf16[3,1024,2048]{2,1,0:T(8,128)(2,1)}, bf16[1,3,2048,512]{3,2,1,0:T(8,128)(2,1)}) %tuple.33), branch_computations={%region_0.0_spmd, %region_1.0_spmd} | conditional | flops 2148007936 | bytes 7340040 | solution.py:411
  140.7 5.1 %convolution_convert_fusion = bf16[1024,512]{1,0:T(8,128)(2,1)} fusion(bf16[3,1024,2048]{2,1,0:T(8,128)(2,1)} %get-tuple-element.42, bf16[3,64,2048]{2,1,0:T(8,128)(2,1)} %get-tuple-element.43, bf16[1,3,64,512]{3,2,1,0:T(8,128)(2,1)S(1)} %get-tuple-element.44), kind=kOutput, calls=%fused_computation.3 | convolution fusion | flops 336134144 | bytes 5570560 | tf_op jit(solution)/shard_map/cond/branch_0_fun/dot_general | solution.py:406
  145.8 3.2 %pad_maximum_fusion.p_ref = bf16[4,4,3,64,512]{4,3,2,1,0:T(8,128)(2,1)} fusion(bf16[4,4,1,64,512]{4,3,2,1,0:T(8,128)(2,1)S(1)} %bitcast.123, bf16[4,4,1,64,512]{4,3,2,1,0:T(8,128)(2,1)S(1)} %bitcast.126, bf16[4,4,1,64,512]{4,3,2,1,0:T(8,128)(2,1)} %bitcast.129), kind=kLoop, calls=%fused_computation.45 | loop fusion | flops 3145728 | bytes 6291456 | tf_op jit(solution)/shard_map/stack | solution.py:412
  149.0 77.2 %shard_map.87 = (bf16[4,2,3,64,1024]{4,3,2,1,0:T(8,128)(2,1)}, bf16[2,192,256]{2,1,0:T(8,128)(2,1)}) custom-call(bf16[4,4,3,64,512]{4,3,2,1,0:T(8,128)(2,1)} %pad_maximum_fusion.p_ref, bf16[192,256]{1,0:T(8,128)(2,1)} %reshape.49.z_ref), custom_call_target="tpu_custom_call" | custom-call | tf_op jit(solution)/shard_map/pallas_call | solution.py:293
  226.2 1.1 copy.22
  227.3 0.2 reshape.50
  227.5 2.7 %subtract_convert_fusion = (bf16[4,64,1024]{2,1,0:T(8,128)(2,1)S(1)}, bf16[4,64,1024]{2,1,0:T(8,128)(2,1)S(1)}, f32[4,64,1024]{2,1,0:T(8,128)S(1)}) fusion(bf16[384,4,64]{0,2,1:T(8,128)(2,1)S(1)} %reshape.50, bf16[4,384,1024]{2,1,0:T(8,128)(2,1)} %bitcast.117), kind=kOutput, calls=%fused_computation.63 | convolution fusion | flops 202375168 | bytes 5439488 | tf_op jit(solution)/shard_map/ajs,jal->jsl/dot_general | solution.py:419
  230.3 1.1 fusion.86
  231.4 0.8 slice_add_fusion.1.cross_ref
  232.2 1.7 convolution_multiply_fusion.1.gram_ref
  233.9 15.4 %shard_map.88 = (f32[4,64,64]{2,1,0:T(8,128)}, f32[4,64,384]{2,1,0:T(8,128)}) custom-call(f32[4,64,64]{2,1,0:T(8,128)} %convolution_multiply_fusion.1.gram_ref, f32[4,64,384]{2,1,0:T(8,128)} %slice_add_fusion.1.cross_ref), custom_call_target="tpu_custom_call" | custom-call | tf_op jit(solution)/shard_map/pallas_call | solution.py:341
  249.3 2.9 %convolution_bitcast_fusion = f32[1,4,64,1024]{3,2,1,0:T(8,128)} fusion(f32[4,64,64]{2,1,0:T(8,128)} %get-tuple-element.72, f32[4,64,1024]{2,1,0:T(8,128)S(1)} %get-tuple-element.82), kind=kOutput, calls=%fused_computation.51 | convolution fusion | flops 201326592 | bytes 2162688 | tf_op jit(solution)/shard_map/jst,jtl->jsl/dot_general | solution.py:427
  252.2 1.5 subtract_convert_fusion.1
  253.8 0.2 copy.23
  254.0 2.7 %fusion.76 = f32[4,128,1024]{2,1,0:T(8,128)S(1)} fusion(bf16[4,128,6,64]{1,3,2,0:T(8,128)(2,1)S(1)} %bitcast.120, bf16[6,4,64,1024]{3,2,1,0:T(8,128)(2,1)} %bitcast.119), kind=kOutput, calls=%fused_computation.50 | convolution fusion | flops 402653184 | bytes 5636096 | tf_op jit(solution)/shard_map/jskr,kjrl->jsl/dot_general | solution.py:433
  256.7 1.1 fusion.85
  (8 shorter events, 0.3 us)
Async XLA Ops:
  0.6 125.8 %copy-start = (bf16[4,64,2048]{2,1,0:T(8,128)(2,1)S(1)}, bf16[4,64,2048]{2,1,0:T(8,128)(2,1)}, u32[]{:S(2)}) copy-start(bf16[4,64,2048]{2,1,0:T(8,128)(2,1)} %param.19) | copy-start | bytes 3145732
  126.4 3.9 %copy-start.2 = (bf16[1,3,64,512]{3,2,1,0:T(8,128)(2,1)S(1)}, bf16[1,3,64,512]{3,2,1,0:T(8,128)(2,1)}, u32[]{:S(2)}) copy-start(bf16[1,3,64,512]{3,2,1,0:T(8,128)(2,1)} %param.14) | copy-start | bytes 589828
  227.5 2.8 %copy-start.1 = (bf16[4,2,3,64,1024]{4,3,2,1,0:T(8,128)(2,1)S(1)}, bf16[4,2,3,64,1024]{4,3,2,1,0:T(8,128)(2,1)}, u32[]{:S(2)}) copy-start(bf16[4,2,3,64,1024]{4,3,2,1,0:T(8,128)(2,1)} %get-tuple-element.71) | copy-start | bytes 9437188
